TPU v7x, 32 devices: a whole 2x2x4 slice. The times are simulated.
32 devices in a mesh: pairs: 8 (over y, x, core), aux: 4 (over z).
Axes of the slice: x: 2, y: 2, z: 4, core: 2. Of those that a mesh axis runs over, the one named last changes fastest.
Arguments:
- panels: bfloat16 [64, 3584, 256], P(None, ('pairs', 'aux')), may hold values from -0.59765625 to 0.59765625
- domain: int32 [8, 6], replicated, may hold values from 0 to 63, as said below
- pair_slots: int32 [96, 2], P('pairs'), may hold values from 0 to 5
- ranks: int32 [96, 2], P('pairs'), may hold values from 40 to 128
- transforms: bfloat16 [96, 2, 256, 128], P('pairs'), may hold values from -0.375 to 0.375
- trial: bfloat16 [96, 2, 128, 128], P('pairs'), may hold values from -0.5 to 0.5
Outputs:
- sigma: bfloat16 [96, 2, 128, 128], P('pairs', None, 'aux')
Inputs may be any that keep to these rules, and one draw needn't show every extreme that they name: `domain`: each row holds 6 different LMO numbers.
All inputs are finite; a program needn't handle non-finite values.
Results may differ from a plain program's by a relative error of at most 0.0039.
Values may be sent and summed in bfloat16 or wider, within the bound.
A program may use at most 128 MiB of HBM per device.

v0:
```python
import jax
import jax.numpy as jnp
from jax import lax
from jax.sharding import PartitionSpec as P

ROOTS = 2


def per_device(panels, domain, pair_slots, ranks, transforms, trial):
    outgoing = jnp.take(panels, domain.reshape(-1), axis=0)
    received = lax.all_to_all(outgoing, "pairs", split_axis=0, concat_axis=1, tiled=True)
    width = transforms.shape[3]
    positions = lax.broadcasted_iota(jnp.int32, ranks.shape + (width,), 2)
    keep = positions < ranks[:, :, None]
    masked_d = jnp.where(keep[:, :, None, :], transforms, jnp.zeros_like(transforms))
    both_keep = keep[:, :, :, None] & keep[:, :, None, :]
    masked_c = jnp.where(both_keep, trial, jnp.zeros_like(trial)).astype(jnp.float32)

    def one_pair(operands):
        slots, coeffs, amplitude = operands
        left = lax.dynamic_index_in_dim(received, slots[0], 0, keepdims=False)
        right = lax.dynamic_index_in_dim(received, slots[1], 0, keepdims=False)
        left_proj = jnp.dot(left, coeffs, preferred_element_type=jnp.float32).astype(jnp.bfloat16)
        right_proj = jnp.dot(right, coeffs, preferred_element_type=jnp.float32).astype(jnp.bfloat16)
        kmat = jnp.einsum("qa,qb->ab", left_proj, right_proj, preferred_element_type=jnp.float32)
        with_right = jnp.dot(kmat, amplitude, precision=lax.Precision.HIGHEST)
        with_left = jnp.einsum("ac,bc->ab", amplitude, kmat, precision=lax.Precision.HIGHEST)
        return kmat + with_right + with_left

    pieces = []
    for root in range(ROOTS):
        pieces.append(
            lax.psum_scatter(
                lax.map(one_pair, (pair_slots, masked_d[:, root], masked_c[:, root])),
                "aux",
                scatter_dimension=1,
                tiled=True,
            )
        )
    summed = jnp.stack(pieces, axis=1)
    return summed.astype(jnp.bfloat16)


def solution(mesh):
    return jax.shard_map(
        per_device,
        mesh=mesh,
        in_specs=(
            P(None, ("pairs", "aux"), None),
            P(),
            P("pairs", None),
            P("pairs", None),
            P("pairs", None, None, None),
            P("pairs", None, None, None),
        ),
        out_specs=P("pairs", None, "aux", None),
        check_vma=False,
    )
```

profile of v0, /device:TPU:0, one launch (start us, length us, event | category | flops | bytes accessed | tf_op | source)
XLA Modules:
  0.0 320.3 jit_solution(12896424059265683317)
XLA Ops:
  8.1 2.8 gather_fusion
  10.9 1.8 broadcast_select_fusion
  12.7 5.3 %all-to-all-start = ((bf16[48,112,256]{2,1,0:T(8,128)(2,1)}), bf16[48,112,256]{2,1,0:T(8,128)(2,1)S(1)}, u32[]{:S(2)}, u32[]{:S(2)}) async-start(bf16[48,112,256]{2,1,0:T(8,128)(2,1)} %broadcast_select_fusion), calls=%async_computation | async-start | bytes 5505024 | tf_op jit(solution)/shard_map/all_to_all | solution.py:11
  18.2 1.6 copy_select_fusion
  19.8 1.3 slice_bitcast_fusion.3
  21.5 1.3 slice_bitcast_fusion.2
  22.8 28.9 %all-to-all-done = bf16[48,112,256]{2,1,0:T(8,128)(2,1)S(1)} async-done(((bf16[48,112,256]{2,1,0:T(8,128)(2,1)}), bf16[48,112,256]{2,1,0:T(8,128)(2,1)S(1)}, u32[]{:S(2)}, u32[]{:S(2)}) %all-to-all-start) | async-done | bytes 2752544 | tf_op jit(solution)/shard_map/all_to_all | solution.py:11
  51.7 1.5 copy-done
  53.2 2.0 copy.7
  56.2 114.3 %while.21 = (s32[]{:T(128)}, f32[12,128,128]{2,1,0:T(8,128)}, s32[12,2]{0,1:T(2,128)S(1)}, bf16[6,896,256]{2,1,0:T(8,128)(2,1)S(1)}, bf16[12,256,128]{2,1,0:T(8,...) while((s32[]{:T(128)}, f32[12,128,128]{2,1,0:T(8,128)}, s32[12,2]{0,1:T(2,128)S(1)}, ...), condition=%wide.region_4.5_spmd, body=%wide.region_3.4_spmd.sunk | while | flops 197394432 | bytes 2098401 | solution.py:34
  61.6 1.4 fusion.111
  64.1 1.7 fusion.113
  68.1 1.1 convolution_convert_fusion.7
  71.1 1.4 fusion.111
  73.6 1.7 fusion.113
  80.6 1.4 fusion.111
  83.2 1.7 fusion.113
  90.2 1.4 fusion.111
  92.7 1.7 fusion.113
  99.7 1.4 fusion.111
  102.2 1.7 fusion.113
  109.2 1.4 fusion.111
  111.7 1.7 fusion.113
  118.7 1.4 fusion.111
  121.2 1.7 fusion.113
  128.3 1.4 fusion.111
  130.8 1.7 fusion.113
  137.8 1.4 fusion.111
  140.3 1.7 fusion.113
  147.3 1.4 fusion.111
  149.8 1.7 fusion.113
  153.8 1.1 convolution_convert_fusion.7
  156.8 1.4 fusion.111
  159.3 1.7 fusion.113
  166.4 1.4 fusion.111
  168.9 1.7 fusion.113
  171.6 117.4 %while.20 = (s32[]{:T(128)}, f32[12,128,128]{2,1,0:T(8,128)}, s32[12,2]{0,1:T(2,128)S(1)}, bf16[6,896,256]{2,1,0:T(8,128)(2,1)S(1)}, bf16[12,256,128]{2,1,0:T(8,...) while((s32[]{:T(128)}, f32[12,128,128]{2,1,0:T(8,128)}, s32[12,2]{0,1:T(2,128)S(1)}, ...), condition=%wide.region_1.2_spmd, body=%wide.region_0.1_spmd.sunk | while | flops 197394432 | bytes 2098401 | solution.py:34
  177.2 1.4 fusion.98
  179.7 1.7 fusion.100
  187.0 1.4 fusion.98
  189.5 1.7 fusion.100
  196.8 1.4 fusion.98
  199.3 1.7 fusion.100
  206.5 1.4 fusion.98
  209.0 1.7 fusion.100
  216.3 1.4 fusion.98
  218.8 1.7 fusion.100
  226.1 1.4 fusion.98
  228.6 1.7 fusion.100
  235.9 1.4 fusion.98
  238.4 1.7 fusion.100
  245.7 1.4 fusion.98
  248.2 1.7 fusion.100
  255.4 1.4 fusion.98
  258.0 1.7 fusion.100
  262.2 1.1 convolution_convert_fusion.6
  265.2 1.4 fusion.98
  267.8 1.7 fusion.100
  275.0 1.4 fusion.98
  277.5 1.7 fusion.100
  281.7 1.1 convolution_convert_fusion.6
  284.8 1.4 fusion.98
  287.3 1.7 fusion.100
  290.0 21.8 %reduce-scatter.3.cloned.1.call-done = f32[12,32,128]{2,1,0:T(8,128)} async-done(((f32[12,128,128]{2,1,0:T(8,128)}), f32[12,32,128]{2,1,0:T(8,128)}) %reduce-scatter.3.cloned.1.call-update) | async-done | bytes 196624 | tf_op jit(solution)/shard_map/reduce_scatter | solution.py:33
  (116 shorter events, 70.9 us)
Async XLA Ops:
  12.7 5.4 %copy-start.3 = (s32[12,2]{0,1:T(2,128)S(1)}, s32[12,2]{0,1:T(2,128)}, u32[]{:S(2)}) copy-start(s32[12,2]{0,1:T(2,128)} %param.13) | copy-start | bytes 292
  12.7 39.0 %all-to-all-start = ((bf16[48,112,256]{2,1,0:T(8,128)(2,1)}), bf16[48,112,256]{2,1,0:T(8,128)(2,1)S(1)}, u32[]{:S(2)}, u32[]{:S(2)}) async-start(bf16[48,112,256]{2,1,0:T(8,128)(2,1)} %broadcast_select_fusion), calls=%async_computation | async-start | bytes 5505024 | tf_op jit(solution)/shard_map/all_to_all | solution.py:11
  18.0 271.0 %reduce-scatter.5.cloned.1.call-start = ((), (), s32[]{:S(2)}) async-start(), calls=%async_computation.4 | async-start | bytes 983040 | tf_op jit(solution)/shard_map/reduce_scatter | solution.py:33
  18.2 2.9 copy-start.1
  51.7 1.5 copy-start
  53.2 3.0 copy-start.2
  170.6 141.2 %reduce-scatter.3.cloned.1.call-start = ((), (), s32[]{:S(2)}) async-start(), calls=%async_computation.3 | async-start | bytes 983040 | tf_op jit(solution)/shard_map/reduce_scatter | solution.py:33
Sparse Core Ops, SparseCore 0:
  170.7 22.5 reduce-scatter.4
  289.2 22.6 reduce-scatter.2
where the time goes:
time: 326 us; the launch traced here: 320 us
  matrix products  127 us (39%)
  loops' own time  89.5 us (27%)
  waiting for transfers between devices  50.8 us (16%)
  local copies, waits for them, and re-layouts  27.5 us (8%)
  between operations  13.5 us (4%)
  other arithmetic  6.59 us (2%)
  starting transfers between devices  5.41 us (2%)
    another operation x2, loops' own time, per_device(): lax.map(one_pair, (pair_slots, masked_d[:, root], masked_c[:, root]))  89.5 us
    dot_general x24, matrix products, one_pair(): with_right = jnp.dot(kmat, amplitude, precision=lax.Precision.HIGHEST)  40.2 us
    dot_general x24, matrix products, one_pair(): jnp.einsum('qa,qb->ab', left_proj, right_proj, preferred_element_type=jnp...  33.5 us
    all_to_all x1, waiting for transfers between devices, per_device(): lax.all_to_all(outgoing, 'pairs', split_axis=0, concat_axis=1, tiled=True)  28.9 us
    dot_general x24, matrix products, one_pair(): jnp.dot(right, coeffs, preferred_element_type=jnp.float32)  26.7 us
    dot_general x24, matrix products, one_pair(): jnp.einsum('ac,bc->ab', amplitude, kmat, precision=lax.Precision.HIGHEST)  26.6 us
    reduce_scatter x2, waiting for transfers between devices, per_device(): lax.psum_scatter(lax.map(one_pair, (pair_slots, masked_d[:, root], masked...  21.8 us
    slice x24, local copies, waits for them, and re-layouts, one_pair(): left = lax.dynamic_index_in_dim(received, slots[0], 0, keepdims=False)  13.5 us
  transfers between devices with their start and end apart: 3, of which 2 were waited for; matrix products, arithmetic and copies ran while one was open for 24% of the time, Pallas kernels for 0%

commit v1 on v0

v1 whole, which is shorter than its diff:
```python
import jax
import jax.numpy as jnp
from jax import lax
from jax.experimental import pallas as pl
from jax.experimental.pallas import tpu as pltpu
from jax.sharding import PartitionSpec as P


def pair_kernel(slots_ref, ranks_ref, panels_ref, d_ref, c_ref, out_ref):
    pair = pl.program_id(0)
    left_slot = slots_ref[pair, 0]
    right_slot = slots_ref[pair, 1]
    roots = d_ref.shape[1]
    width = d_ref.shape[3]
    columns = lax.broadcasted_iota(jnp.int32, (1, width), 1)
    rows = lax.broadcasted_iota(jnp.int32, (width, 1), 0)
    masked = []
    for root in range(roots):
        rank = ranks_ref[pair, root]
        masked.append(jnp.where(columns < rank, d_ref[0, root], jnp.zeros((), d_ref.dtype)))
    coeffs = jnp.concatenate(masked, axis=1)
    left = jnp.dot(panels_ref[left_slot], coeffs, preferred_element_type=jnp.float32).astype(jnp.bfloat16)
    right = jnp.dot(panels_ref[right_slot], coeffs, preferred_element_type=jnp.float32).astype(jnp.bfloat16)
    for root in range(roots):
        rank = ranks_ref[pair, root]
        part = slice(root * width, (root + 1) * width)
        kmat = lax.dot_general(
            left[:, part], right[:, part], (((0,), (0,)), ((), ())), preferred_element_type=jnp.float32
        )
        keep = (columns < rank) & (rows < rank)
        amplitude = jnp.where(keep, c_ref[0, root], jnp.zeros((), c_ref.dtype))
        rounded = kmat.astype(jnp.bfloat16)
        with_right = jnp.dot(rounded, amplitude, preferred_element_type=jnp.float32)
        with_left = lax.dot_general(
            amplitude, rounded, (((1,), (1,)), ((), ())), preferred_element_type=jnp.float32
        )
        out_ref[0, root] = kmat + with_right + with_left


def per_device(panels, domain, pair_slots, ranks, transforms, trial):
    outgoing = panels.at[domain.reshape(-1)].get(mode="promise_in_bounds")
    received = lax.all_to_all(outgoing, "pairs", split_axis=0, concat_axis=1, tiled=True)
    pairs, roots, nv, width = transforms.shape
    slots, rows, _ = received.shape
    partial = pl.pallas_call(
        pair_kernel,
        grid=(pairs,),
        in_specs=[
            pl.BlockSpec(memory_space=pltpu.SMEM),
            pl.BlockSpec(memory_space=pltpu.SMEM),
            pl.BlockSpec((slots, rows, nv), lambda p: (0, 0, 0)),
            pl.BlockSpec((1, roots, nv, width), lambda p: (p, 0, 0, 0)),
            pl.BlockSpec((1, roots, width, width), lambda p: (p, 0, 0, 0)),
        ],
        out_specs=pl.BlockSpec((1, roots, width, width), lambda p: (p, 0, 0, 0)),
        out_shape=jax.ShapeDtypeStruct((pairs, roots, width, width), jnp.float32),
    )(pair_slots, ranks, received, transforms, trial)
    summed = lax.psum_scatter(partial, "aux", scatter_dimension=2, tiled=True)
    return summed.astype(jnp.bfloat16)


def solution(mesh):
    return jax.shard_map(
        per_device,
        mesh=mesh,
        in_specs=(
            P(None, ("pairs", "aux"), None),
            P(),
            P("pairs", None),
            P("pairs", None),
            P("pairs", None, None, None),
            P("pairs", None, None, None),
        ),
        out_specs=P("pairs", None, "aux", None),
        check_vma=False,
    )
```

time: 326 us -> 111 us (0.34); the launches traced: 320 us -> 110 us
  matrix products: 127 us -> 0 us
  loops' own time: 89.5 us -> 0 us
  local copies, waits for them, and re-layouts: 27.5 us -> 8.35 us
  waiting for transfers between devices: 50.8 us -> 67.2 us
  Pallas kernels: 0 us -> 14.3 us
  other arithmetic: 6.59 us -> 1.72 us
    dot_general x96 -> x0, matrix products: 127 us -> none  [the longest x24 40.2 us: one_pair(): with_right = jnp.dot(kmat, amplitude, precision=lax.Precision.HIGHEST)]
    another operation x2 -> x0, loops' own time: 89.5 us -> none  [per_device(): lax.map(one_pair, (pair_slots, masked_d[:, root], masked_c[:, root]))]
    pallas_call x0 -> x1, Pallas kernels: none -> 14.3 us  [per_device(): pl.pallas_call(pair_kernel, grid=(pairs,), in_specs=[pl.BlockSpec(memory_...]
    slice x24 -> x0, local copies, waits for them, and re-layouts: 13.5 us -> none  [one_pair(): left = lax.dynamic_index_in_dim(received, slots[0], 0, keepdims=False)]
    reduce_scatter x2 -> x1, waiting for transfers between devices: 21.8 us -> 35 us  [per_device(): summed = lax.psum_scatter(partial, 'aux', scatter_dimension=2, tiled=True)]
    select_n x3 -> x1, other arithmetic: 3.45 us -> 0.01 us  [per_device(): outgoing = panels.at[domain.reshape(-1)].get(mode='promise_in_bounds')]
    all_to_all x1, waiting for transfers between devices: 28.9 us -> 32.2 us  [per_device(): lax.all_to_all(outgoing, 'pairs', split_axis=0, concat_axis=1, tiled=True)]
  transfers between devices with their start and end apart: 3 -> 2, of which waited for: 2 -> 2; matrix products, arithmetic and copies ran while one was open for 24% -> 1% of each run, Pallas kernels for 0% -> 0%
where the time goes in v1:
time: 111 us; the launch traced here: 110 us
  waiting for transfers between devices  67.2 us (61%)
  Pallas kernels  14.3 us (13%)
  between operations  13.4 us (12%)
  local copies, waits for them, and re-layouts  8.35 us (8%)
  starting transfers between devices  5.37 us (5%)
  other arithmetic  1.72 us (2%)
    reduce_scatter x1, waiting for transfers between devices, per_device(): summed = lax.psum_scatter(partial, 'aux', scatter_dimension=2, tiled=True)  35 us
    all_to_all x1, waiting for transfers between devices, per_device(): lax.all_to_all(outgoing, 'pairs', split_axis=0, concat_axis=1, tiled=True)  32.2 us
    pallas_call x1, Pallas kernels, per_device(): pl.pallas_call(pair_kernel, grid=(pairs,), in_specs=[pl.BlockSpec(memory_...  14.3 us
    all_to_all x1, starting transfers between devices, per_device(): lax.all_to_all(outgoing, 'pairs', split_axis=0, concat_axis=1, tiled=True)  5.33 us
    gather x1, local copies, waits for them, and re-layouts, per_device(): outgoing = panels.at[domain.reshape(-1)].get(mode='promise_in_bounds')  4.41 us
  transfers between devices with their start and end apart: 2, of which 2 were waited for; matrix products, arithmetic and copies ran while one was open for 1% of the time, Pallas kernels for 0%

profile of v1, /device:TPU:0, one launch (start us, length us, event | category | flops | bytes accessed | tf_op | source)
XLA Modules:
  0.0 110.3 jit_solution(8356804969943616494)
XLA Ops:
  6.5 0.8 reshape.31
  7.3 4.4 %gather_fusion = bf16[48,112,256]{2,1,0:T(8,128)(2,1)} fusion(bf16[64,112,256]{2,1,0:T(8,128)(2,1)} %param.6, s32[1024]{0:T(1024)S(1)} %pad_clamp_fusion), kind=kCustom, calls=%fused_computation | custom fusion | bytes 5505216 | tf_op jit(solution)/shard_map/gather | solution.py:41
  11.7 0.0 copy-start
  11.7 0.0 copy-start.1
  11.7 5.3 %all-to-all-start = ((bf16[48,112,256]{2,1,0:T(8,128)(2,1)}), bf16[48,112,256]{2,1,0:T(8,128)(2,1)S(1)}, u32[]{:S(2)}, u32[]{:S(2)}) async-start(bf16[48,112,256]{2,1,0:T(8,128)(2,1)} %gather_fusion), calls=%async_computation | async-start | bytes 5505024 | tf_op jit(solution)/shard_map/all_to_all | solution.py:42
  17.1 0.0 reduce-scatter.2.cloned.1.call-start
  17.1 0.0 copy-done
  17.1 0.7 copy.8.slots_ref
  17.8 0.0 copy-done.1
  17.8 0.7 copy.9.ranks_ref
  18.5 32.2 %all-to-all-done = bf16[48,112,256]{2,1,0:T(8,128)(2,1)S(1)} async-done(((bf16[48,112,256]{2,1,0:T(8,128)(2,1)}), bf16[48,112,256]{2,1,0:T(8,128)(2,1)S(1)}, u32[]{:S(2)}, u32[]{:S(2)}) %all-to-all-start) | async-done | bytes 2752544 | tf_op jit(solution)/shard_map/all_to_all | solution.py:42
  50.7 1.8 %copy.7 = bf16[8,6,112,256]{3,2,0,1:T(8,128)(2,1)} copy(bf16[8,6,112,256]{3,2,1,0:T(8,128)(2,1)S(1)} %bitcast.7) | data formatting | bytes 5505024 | tf_op jit(solution)/shard_map/all_to_all | solution.py:42
  52.5 14.3 %shard_map.64 = f32[12,2,128,128]{3,2,1,0:T(8,128)} custom-call(s32[12,2]{1,0:T(8,128)} %copy.8.slots_ref, s32[12,2]{1,0:T(8,128)} %copy.9.ranks_ref, bf16[6,896,256]{2,1,0:T(8,128)(2,1)} %bitcast.6, bf16[12,2,256,128]{3,2,1,0:T(8,128)(2,1)} %d_ref.1, bf16[12,2,128,128]{3,2,1,0:T(8,128)(2,1)} %c_ref.1), custom_call_target="tpu_custom_call" | custom-call | tf_op jit(solution)/shard_map/pallas_call | solution.py:45
  66.8 0.0 reduce-scatter.2.cloned.1.call-update
  66.8 35.0 %reduce-scatter.2.cloned.1.call-done = f32[12,2,32,128]{3,2,1,0:T(8,128)} async-done(((f32[12,2,128,128]{3,2,1,0:T(8,128)}), f32[12,2,32,128]{3,2,1,0:T(8,128)}) %reduce-scatter.2.cloned.1.call-update) | async-done | bytes 393232 | tf_op jit(solution)/shard_map/reduce_scatter | solution.py:58
  101.8 1.7 %convert_element_type.3 = bf16[12,2,32,128]{3,2,1,0:T(8,128)(2,1)} convert(f32[12,2,32,128]{3,2,1,0:T(8,128)} %reduce-scatter.2.cloned.1.call-done) | non-fusion elementwise | flops 98304 | bytes 589824 | tf_op jit(solution)/shard_map/convert_element_type | solution.py:59
  (2 shorter events, 0.0 us)
Async XLA Ops:
  11.7 5.4 %copy-start = (s32[12,2]{0,1:T(2,128)S(1)}, s32[12,2]{0,1:T(2,128)}, u32[]{:S(2)}) copy-start(s32[12,2]{0,1:T(2,128)} %param.8) | copy-start | bytes 292
  11.7 6.1 %copy-start.1 = (s32[12,2]{0,1:T(2,128)S(1)}, s32[12,2]{0,1:T(2,128)}, u32[]{:S(2)}) copy-start(s32[12,2]{0,1:T(2,128)} %param.9) | copy-start | bytes 292
  11.7 39.0 %all-to-all-start = ((bf16[48,112,256]{2,1,0:T(8,128)(2,1)}), bf16[48,112,256]{2,1,0:T(8,128)(2,1)S(1)}, u32[]{:S(2)}, u32[]{:S(2)}) async-start(bf16[48,112,256]{2,1,0:T(8,128)(2,1)} %gather_fusion), calls=%async_computation | async-start | bytes 5505024 | tf_op jit(solution)/shard_map/all_to_all | solution.py:42
  17.1 84.7 %reduce-scatter.2.cloned.1.call-start = ((), (), s32[]{:S(2)}) async-start(), calls=%async_computation.2 | async-start | bytes 1966080 | tf_op jit(solution)/shard_map/reduce_scatter | solution.py:58
Sparse Core Ops, SparseCore 0:
  66.9 34.8 reduce-scatter.1

commit v2 on v0

v2 whole, which is shorter than its diff:
```python
import functools

import jax
import jax.numpy as jnp
from jax import lax
from jax.experimental import pallas as pl
from jax.experimental.pallas import tpu as pltpu
from jax.sharding import PartitionSpec as P

MESH = pl.DeviceIdType.MESH
CHUNKS = 4


def peer_of(me, offset, count):
    if count & (count - 1):
        return lax.rem(me + offset, count)
    peer = me
    bit = 1
    while bit < count:
        if offset & bit:
            peer = peer + bit * (1 - 2 * lax.rem(me // bit, 2))
        bit *= 2
    return peer


def fused_kernel(
    n, m, lanes, slots_ref, ranks_ref, outgoing_ref, d_ref, c_ref, out_ref,
    d_raw, d_mask, c_raw, acc, send_buf, landed,
    local_sem, send_sem, recv_sem, part_send, part_recv, *received,
):
    me = lax.axis_index("pairs")
    mine = lax.axis_index("aux")
    pairs, roots, nv, width = d_ref.shape
    slots = received[0].shape[0]
    rows = received[0].shape[2]
    strip = width // m
    group = pairs // CHUNKS

    barrier = pltpu.get_barrier_semaphore()
    for offset in range(1, n):
        pl.semaphore_signal(barrier, inc=1, device_id=(peer_of(me, offset, n), mine), device_id_type=MESH)
    for offset in range(1, m):
        pl.semaphore_signal(barrier, inc=1, device_id=(me, lax.rem(mine + offset, m)), device_id_type=MESH)
    own = pltpu.make_async_copy(outgoing_ref.at[pl.ds(me * slots, slots)], received[0].at[:, 0], local_sem.at[0])
    own.start()
    d_copy = pltpu.make_async_copy(d_ref, d_raw, local_sem.at[1])
    d_copy.start()
    c_copy = pltpu.make_async_copy(c_ref, c_raw, local_sem.at[2])
    c_copy.start()
    pl.semaphore_wait(barrier, n + m - 2)

    copies = []
    for offset in range(1, n):
        peer = peer_of(me, offset, n)
        copy = pltpu.make_async_remote_copy(
            src_ref=outgoing_ref.at[pl.ds(peer * slots, slots)],
            dst_ref=received[offset // lanes].at[:, offset % lanes],
            send_sem=send_sem.at[offset],
            recv_sem=recv_sem.at[offset],
            device_id=(peer, mine),
            device_id_type=MESH,
        )
        copy.start()
        copies.append(copy)

    columns = lax.broadcasted_iota(jnp.int32, (1, width), 1)
    row_ids = lax.broadcasted_iota(jnp.int32, (width, 1), 0)
    d_copy.wait()
    c_copy.wait()

    def mask_pair(pair, carry):
        for root in range(roots):
            rank = ranks_ref[pair, root]
            d_mask[pair, :, root * width:(root + 1) * width] = jnp.where(
                columns < rank, d_raw[pair, root], jnp.zeros((), d_raw.dtype)
            )
            keep = (columns < rank) & (row_ids < rank)
            c_raw[pair, root] = jnp.where(keep, c_raw[pair, root], jnp.zeros((), c_raw.dtype))
        return carry

    lax.fori_loop(0, pairs, mask_pair, 0)

    def partial_of(pair, block):
        both = lanes * rows
        left = block[slots_ref[pair, 0]].reshape(both, nv)
        right = block[slots_ref[pair, 1]].reshape(both, nv)
        coeffs = d_mask[pair]
        left = jnp.dot(left, coeffs, preferred_element_type=jnp.float32).astype(jnp.bfloat16)
        right = jnp.dot(right, coeffs, preferred_element_type=jnp.float32).astype(jnp.bfloat16)
        return [
            lax.dot_general(
                left[:, root * width:(root + 1) * width],
                right[:, root * width:(root + 1) * width],
                (((0,), (0,)), ((), ())),
                preferred_element_type=jnp.float32,
            )
            for root in range(roots)
        ]

    stages = len(received)
    for stage in range(stages):
        for lane in range(lanes):
            offset = stage * lanes + lane
            if offset == 0:
                own.wait()
            else:
                copies[offset - 1].wait_recv()
        block = received[stage]
        if stage < stages - 1:

            def accumulate(pair, carry, block=block, stage=stage):
                parts = partial_of(pair, block)
                for root in range(roots):
                    if stage == 0:
                        acc[pair, root] = parts[root]
                    else:
                        acc[pair, root] += parts[root]
                return carry

            lax.fori_loop(0, pairs, accumulate, 0, unroll=2)

    block = received[stages - 1]

    def finish(pair, carry):
        parts = partial_of(pair, block)
        for root in range(roots):
            kmat = parts[root] if stages == 1 else acc[pair, root] + parts[root]
            rounded = kmat.astype(jnp.bfloat16)
            amplitude = c_raw[pair, root]
            with_right = jnp.dot(rounded, amplitude, preferred_element_type=jnp.float32)
            with_left = lax.dot_general(
                amplitude, rounded, (((1,), (1,)), ((), ())), preferred_element_type=jnp.float32
            )
            sigma = kmat + with_right + with_left
            acc[pair, root] = sigma
            for owner in range(m):
                send_buf[owner, pair, root] = sigma[owner * strip:(owner + 1) * strip].astype(jnp.bfloat16)
        return carry

    sums = []
    for chunk in range(CHUNKS):
        lax.fori_loop(chunk * group, (chunk + 1) * group, finish, 0, unroll=group)
        for offset in range(1, m):
            peer = lax.rem(mine + offset, m)
            copy = pltpu.make_async_remote_copy(
                src_ref=send_buf.at[peer, pl.ds(chunk * group, group)],
                dst_ref=landed.at[offset - 1, pl.ds(chunk * group, group)],
                send_sem=part_send.at[chunk, offset],
                recv_sem=part_recv.at[chunk, offset],
                device_id=(me, peer),
                device_id_type=MESH,
            )
            copy.start()
            sums.append((chunk, offset, copy))

    for chunk in range(CHUNKS):
        for at, offset, copy in sums:
            if at == chunk:
                copy.wait_recv()
        part = pl.ds(chunk * group, group)
        total = acc[part, :, pl.ds(mine * strip, strip), :]
        for offset in range(1, m):
            total = total + landed[offset - 1, part].astype(jnp.float32)
        out_ref[part] = total.astype(out_ref.dtype)
    for copy in copies:
        copy.wait_send()
    for _, _, copy in sums:
        copy.wait_send()


def per_device(n, m, panels, domain, pair_slots, ranks, transforms, trial):
    pairs, roots, nv, width = transforms.shape
    slots = domain.shape[1]
    rows = panels.shape[1]
    lanes = 2
    outgoing = panels.at[domain.reshape(-1)].get(mode="promise_in_bounds")
    smem = pl.BlockSpec(memory_space=pltpu.SMEM)
    hbm = pl.BlockSpec(memory_space=pltpu.HBM)
    return pl.pallas_call(
        functools.partial(fused_kernel, n, m, lanes),
        in_specs=[smem, smem, hbm, hbm, hbm],
        out_specs=pl.BlockSpec(memory_space=pltpu.VMEM),
        out_shape=jax.ShapeDtypeStruct((pairs, roots, width // m, width), jnp.bfloat16),
        scratch_shapes=[
            pltpu.VMEM((pairs, roots, nv, width), transforms.dtype),
            pltpu.VMEM((pairs, nv, roots * width), transforms.dtype),
            pltpu.VMEM((pairs, roots, width, width), trial.dtype),
            pltpu.VMEM((pairs, roots, width, width), jnp.float32),
            pltpu.VMEM((m, pairs, roots, width // m, width), jnp.bfloat16),
            pltpu.VMEM((m - 1, pairs, roots, width // m, width), jnp.bfloat16),
            pltpu.SemaphoreType.DMA((3,)),
            pltpu.SemaphoreType.DMA((n,)),
            pltpu.SemaphoreType.DMA((n,)),
            pltpu.SemaphoreType.DMA((CHUNKS, m)),
            pltpu.SemaphoreType.DMA((CHUNKS, m)),
        ]
        + [pltpu.VMEM((slots, lanes, rows, nv), panels.dtype) for _ in range(n // lanes)],
        compiler_params=pltpu.CompilerParams(
            collective_id=0, has_side_effects=True, vmem_limit_bytes=60 * 2**20
        ),
    )(pair_slots, ranks, outgoing, transforms, trial)


def solution(mesh):
    return jax.shard_map(
        functools.partial(per_device, mesh.shape["pairs"], mesh.shape["aux"]),
        mesh=mesh,
        in_specs=(
            P(None, ("pairs", "aux"), None),
            P(),
            P("pairs", None),
            P("pairs", None),
            P("pairs", None, None, None),
            P("pairs", None, None, None),
        ),
        out_specs=P("pairs", None, "aux", None),
        check_vma=False,
    )
```

time: 326 us -> 67.6 us (0.21); the launches traced: 320 us -> 67.3 us
  matrix products: 127 us -> 0 us
  loops' own time: 89.5 us -> 0 us
  Pallas kernels: 0 us -> 57.8 us
  waiting for transfers between devices: 50.8 us -> 0 us
  local copies, waits for them, and re-layouts: 27.5 us -> 9.51 us
  between operations: 13.5 us -> 0.01 us
  other arithmetic: 6.59 us -> 0.01 us
  starting transfers between devices: 5.41 us -> 0 us
    dot_general x96 -> x0, matrix products: 127 us -> none  [the longest x24 40.2 us: one_pair(): with_right = jnp.dot(kmat, amplitude, precision=lax.Precision.HIGHEST)]
    another operation x2 -> x0, loops' own time: 89.5 us -> none  [per_device(): lax.map(one_pair, (pair_slots, masked_d[:, root], masked_c[:, root]))]
    pallas_call x0 -> x1, Pallas kernels: none -> 57.8 us  [per_device(): pl.pallas_call(functools.partial(fused_kernel, n, m, lanes), in_specs=[sm...]
    all_to_all x1 -> x0, waiting for transfers between devices: 28.9 us -> none  [per_device(): lax.all_to_all(outgoing, 'pairs', split_axis=0, concat_axis=1, tiled=True)]
    reduce_scatter x2 -> x0, waiting for transfers between devices: 21.8 us -> none  [per_device(): lax.psum_scatter(lax.map(one_pair, (pair_slots, masked_d[:, root], masked...]
    slice x24 -> x0, local copies, waits for them, and re-layouts: 13.5 us -> none  [one_pair(): left = lax.dynamic_index_in_dim(received, slots[0], 0, keepdims=False)]
    all_to_all x1 -> x0, starting transfers between devices: 5.33 us -> none  [per_device(): lax.all_to_all(outgoing, 'pairs', split_axis=0, concat_axis=1, tiled=True)]
    select_n x3 -> x1, other arithmetic: 3.45 us -> 0.01 us  [per_device(): outgoing = panels.at[domain.reshape(-1)].get(mode='promise_in_bounds')]
  transfers between devices with their start and end apart: 3 -> 0, of which waited for: 2 -> 0; matrix products, arithmetic and copies ran while one was open for 24% -> 0% of each run, Pallas kernels for 0% -> 0%
where the time goes in v2:
time: 67.6 us; the launch traced here: 67.3 us
  Pallas kernels  57.8 us (86%)
  local copies, waits for them, and re-layouts  9.51 us (14%)
    pallas_call x1, Pallas kernels, per_device(): pl.pallas_call(functools.partial(fused_kernel, n, m, lanes), in_specs=[sm...  57.8 us
    gather x1, local copies, waits for them, and re-layouts, per_device(): outgoing = panels.at[domain.reshape(-1)].get(mode='promise_in_bounds')  4.41 us
    unnamed x3, local copies, waits for them, and re-layouts  4.33 us

profile of v2, /device:TPU:0, one launch (start us, length us, event | category | flops | bytes accessed | tf_op | source)
XLA Modules:
  0.0 67.3 jit_solution(17277825055108231118)
XLA Ops:
  0.0 0.8 %reshape.31 = s32[48,1]{0,1:T(1,128)S(1)} reshape(s32[8,6]{1,0:T(8,128)} %param.7) | data formatting | bytes 384 | tf_op jit(solution)/shard_map/reshape | solution.py:176
  0.8 1.4 %copy.7.slots_ref = s32[12,2]{1,0:T(8,128)} copy(s32[12,2]{0,1:T(2,128)} %param.8) | data formatting | bytes 192 | tf_op args[2]
  2.1 1.4 %copy.8.ranks_ref = s32[12,2]{1,0:T(8,128)} copy(s32[12,2]{0,1:T(2,128)} %param.9) | data formatting | bytes 192 | tf_op args[3]
  3.5 4.4 %gather_fusion = bf16[48,112,256]{2,1,0:T(8,128)(2,1)} fusion(bf16[64,112,256]{2,1,0:T(8,128)(2,1)} %param.6, s32[1024]{0:T(1024)S(1)} %pad_clamp_fusion), kind=kCustom, calls=%fused_computation | custom fusion | bytes 5505216 | tf_op jit(solution)/shard_map/gather | solution.py:176
  7.9 57.8 %shard_map.64 = bf16[12,2,32,128]{3,2,1,0:T(8,128)(2,1)} custom-call(s32[12,2]{1,0:T(8,128)} %copy.7.slots_ref, s32[12,2]{1,0:T(8,128)} %copy.8.ranks_ref, bf16[48,112,256]{2,1,0:T(8,128)(2,1)} %gather_fusion, bf16[12,2,256,128]{3,2,1,0:T(8,128)(2,1)} %d_ref.1, bf16[12,2,128,128]{3,2,1,0:T(8,128)(2,1)} %c_ref.1), custom_call_target="tpu_custom_call" | custom-call | tf_op jit(solution)/shard_map/pallas_call | solution.py:179
  65.7 1.6 %copy.10 = bf16[12,2,32,128]{3,2,1,0:T(8,128)(2,1)} copy(bf16[12,2,32,128]{3,2,1,0:T(8,128)(2,1)} %shard_map.64) | data formatting | bytes 393216
  (2 shorter events, 0.0 us)

commit v3 on v2

--- a/solution.py
+++ b/solution.py
@@ -24,8 +24,8 @@
 
 
 def fused_kernel(
-    n, m, lanes, slots_ref, ranks_ref, outgoing_ref, d_ref, c_ref, out_ref,
-    d_raw, d_mask, c_raw, acc, send_buf, landed,
+    n, m, plan, domain_ref, slots_ref, ranks_ref, panels_ref, d_ref, c_ref, out_ref,
+    panels, outgoing, d_raw, d_mask, c_raw, acc, send_buf, landed,
     local_sem, send_sem, recv_sem, part_send, part_recv, *received,
 ):
     me = lax.axis_index("pairs")
@@ -41,27 +41,35 @@
         pl.semaphore_signal(barrier, inc=1, device_id=(peer_of(me, offset, n), mine), device_id_type=MESH)
     for offset in range(1, m):
         pl.semaphore_signal(barrier, inc=1, device_id=(me, lax.rem(mine + offset, m)), device_id_type=MESH)
-    own = pltpu.make_async_copy(outgoing_ref.at[pl.ds(me * slots, slots)], received[0].at[:, 0], local_sem.at[0])
-    own.start()
+    panels_copy = pltpu.make_async_copy(panels_ref, panels, local_sem.at[0])
+    panels_copy.start()
     d_copy = pltpu.make_async_copy(d_ref, d_raw, local_sem.at[1])
     d_copy.start()
     c_copy = pltpu.make_async_copy(c_ref, c_raw, local_sem.at[2])
     c_copy.start()
     pl.semaphore_wait(barrier, n + m - 2)
 
-    copies = []
+    panels_copy.wait()
+    place = {offset: (stage, lane) for stage, group in enumerate(plan) for lane, offset in enumerate(group)}
+    copies = {}
     for offset in range(1, n):
         peer = peer_of(me, offset, n)
-        copy = pltpu.make_async_remote_copy(
-            src_ref=outgoing_ref.at[pl.ds(peer * slots, slots)],
-            dst_ref=received[offset // lanes].at[:, offset % lanes],
+        for slot in range(slots):
+            outgoing[offset - 1, slot] = panels[domain_ref[peer, slot]]
+        stage, lane = place[offset]
+        copies[offset] = pltpu.make_async_remote_copy(
+            src_ref=outgoing.at[offset - 1],
+            dst_ref=received[stage].at[:, lane],
             send_sem=send_sem.at[offset],
             recv_sem=recv_sem.at[offset],
             device_id=(peer, mine),
             device_id_type=MESH,
         )
-        copy.start()
-        copies.append(copy)
+        if offset > 1:
+            copies[offset - 1].start()
+    for slot in range(slots):
+        received[0][slot, 0] = panels[domain_ref[me, slot]]
+    copies[n - 1].start()
 
     columns = lax.broadcasted_iota(jnp.int32, (1, width), 1)
     row_ids = lax.broadcasted_iota(jnp.int32, (width, 1), 0)
@@ -70,7 +78,7 @@
 
     def mask_pair(pair, carry):
         for root in range(roots):
-            rank = ranks_ref[pair, root]
+            rank = ranks_ref[root, pair]
             d_mask[pair, :, root * width:(root + 1) * width] = jnp.where(
                 columns < rank, d_raw[pair, root], jnp.zeros((), d_raw.dtype)
             )
@@ -81,9 +89,9 @@
     lax.fori_loop(0, pairs, mask_pair, 0)
 
     def partial_of(pair, block):
-        both = lanes * rows
-        left = block[slots_ref[pair, 0]].reshape(both, nv)
-        right = block[slots_ref[pair, 1]].reshape(both, nv)
+        both = block.shape[1] * rows
+        left = block[slots_ref[0, pair]].reshape(both, nv)
+        right = block[slots_ref[1, pair]].reshape(both, nv)
         coeffs = d_mask[pair]
         left = jnp.dot(left, coeffs, preferred_element_type=jnp.float32).astype(jnp.bfloat16)
         right = jnp.dot(right, coeffs, preferred_element_type=jnp.float32).astype(jnp.bfloat16)
@@ -99,12 +107,9 @@
 
     stages = len(received)
     for stage in range(stages):
-        for lane in range(lanes):
-            offset = stage * lanes + lane
-            if offset == 0:
-                own.wait()
-            else:
-                copies[offset - 1].wait_recv()
+        for offset in plan[stage]:
+            if offset:
+                copies[offset].wait_recv()
         block = received[stage]
         if stage < stages - 1:
 
@@ -162,7 +167,7 @@
         for offset in range(1, m):
             total = total + landed[offset - 1, part].astype(jnp.float32)
         out_ref[part] = total.astype(out_ref.dtype)
-    for copy in copies:
+    for copy in copies.values():
         copy.wait_send()
     for _, _, copy in sums:
         copy.wait_send()
@@ -172,16 +177,17 @@
     pairs, roots, nv, width = transforms.shape
     slots = domain.shape[1]
     rows = panels.shape[1]
-    lanes = 2
-    outgoing = panels.at[domain.reshape(-1)].get(mode="promise_in_bounds")
+    plan = [(offset, offset + 1) for offset in range(0, n - 2, 2)] + [(n - 2,), (n - 1,)]
     smem = pl.BlockSpec(memory_space=pltpu.SMEM)
     hbm = pl.BlockSpec(memory_space=pltpu.HBM)
     return pl.pallas_call(
-        functools.partial(fused_kernel, n, m, lanes),
-        in_specs=[smem, smem, hbm, hbm, hbm],
+        functools.partial(fused_kernel, n, m, plan),
+        in_specs=[smem, smem, smem, hbm, hbm, hbm],
         out_specs=pl.BlockSpec(memory_space=pltpu.VMEM),
         out_shape=jax.ShapeDtypeStruct((pairs, roots, width // m, width), jnp.bfloat16),
         scratch_shapes=[
+            pltpu.VMEM(panels.shape, panels.dtype),
+            pltpu.VMEM((n - 1, slots, rows, nv), panels.dtype),
             pltpu.VMEM((pairs, roots, nv, width), transforms.dtype),
             pltpu.VMEM((pairs, nv, roots * width), transforms.dtype),
             pltpu.VMEM((pairs, roots, width, width), trial.dtype),
@@ -194,11 +200,11 @@
             pltpu.SemaphoreType.DMA((CHUNKS, m)),
             pltpu.SemaphoreType.DMA((CHUNKS, m)),
         ]
-        + [pltpu.VMEM((slots, lanes, rows, nv), panels.dtype) for _ in range(n // lanes)],
+        + [pltpu.VMEM((slots, len(group), rows, nv), panels.dtype) for group in plan],
         compiler_params=pltpu.CompilerParams(
             collective_id=0, has_side_effects=True, vmem_limit_bytes=60 * 2**20
         ),
-    )(pair_slots, ranks, outgoing, transforms, trial)
+    )(domain, pair_slots.T, ranks.T, panels, transforms, trial)
 
 
 def solution(mesh):

time: 67.6 us -> 60.5 us (0.89)
  local copies, waits for them, and re-layouts: 9.51 us -> 1.62 us
  Pallas kernels: 57.8 us -> 58.7 us
    gather x1 -> x0, local copies, waits for them, and re-layouts: 4.41 us -> none  [per_device(): outgoing = panels.at[domain.reshape(-1)].get(mode='promise_in_bounds')]
    unnamed x3 -> x1, local copies, waits for them, and re-layouts: 4.33 us -> 1.62 us
    pallas_call x1, Pallas kernels: 57.8 us -> 58.7 us  [per_device(): pl.pallas_call(functools.partial(fused_kernel, n, m, plan), in_specs=[sme...]
    reshape x1 -> x0, local copies, waits for them, and re-layouts: 0.76 us -> none  [per_device(): outgoing = panels.at[domain.reshape(-1)].get(mode='promise_in_bounds')]
where the time goes in v3:
time: 60.5 us; the launch traced here: 60.3 us
  Pallas kernels  58.7 us (97%)
  local copies, waits for them, and re-layouts  1.62 us (3%)
    pallas_call x1, Pallas kernels, per_device(): pl.pallas_call(functools.partial(fused_kernel, n, m, plan), in_specs=[sme...  58.7 us
    unnamed x1, local copies, waits for them, and re-layouts  1.62 us

profile of v3, /device:TPU:0, one launch (start us, length us, event | category | flops | bytes accessed | tf_op | source)
XLA Modules:
  0.0 60.3 jit_solution(6878251924854711098)
XLA Ops:
  0.0 58.7 %shard_map.64 = bf16[12,2,32,128]{3,2,1,0:T(8,128)(2,1)} custom-call(s32[8,6]{1,0:T(8,128)} %domain_ref.1, s32[2,12]{1,0:T(2,128)} %bitcast.2, s32[2,12]{1,0:T(2,128)} %bitcast.3, bf16[64,112,256]{2,1,0:T(8,128)(2,1)} %panels_ref.1, bf16[12,2,256,128]{3,2,1,0:T(8,128)(2,1)} %d_ref.1, bf16[12,2,128,128]{3,2,1,0:T(8,128)(2,1)} %c_ref.1), custom_call_target="tpu_custom_call" | custom-call | tf_op jit(solution)/shard_map/pallas_call | solution.py:183
  58.7 1.6 %copy.8 = bf16[12,2,32,128]{3,2,1,0:T(8,128)(2,1)} copy(bf16[12,2,32,128]{3,2,1,0:T(8,128)(2,1)} %shard_map.64) | data formatting | bytes 393216

commit v4 on v3

--- a/solution.py
+++ b/solution.py
@@ -8,7 +8,7 @@
 from jax.sharding import PartitionSpec as P
 
 MESH = pl.DeviceIdType.MESH
-CHUNKS = 4
+CHUNKS = 6
 
 
 def peer_of(me, offset, count):
@@ -145,7 +145,7 @@
     sums = []
     for chunk in range(CHUNKS):
         lax.fori_loop(chunk * group, (chunk + 1) * group, finish, 0, unroll=group)
-        for offset in range(1, m):
+        for offset in sorted(range(1, m), key=lambda hop: -min(hop, m - hop)):
             peer = lax.rem(mine + offset, m)
             copy = pltpu.make_async_remote_copy(
                 src_ref=send_buf.at[peer, pl.ds(chunk * group, group)],

time: 60.5 us -> 60.6 us (level)
  no operation moved by 1% of the time
where the time goes in v4:
time: 60.6 us; the launch traced here: 60.4 us
  Pallas kernels  58.8 us (97%)
  local copies, waits for them, and re-layouts  1.62 us (3%)
    pallas_call x1, Pallas kernels, per_device(): pl.pallas_call(functools.partial(fused_kernel, n, m, plan), in_specs=[sme...  58.8 us
    unnamed x1, local copies, waits for them, and re-layouts  1.62 us

profile of v4, /device:TPU:0, one launch (start us, length us, event | category | flops | bytes accessed | tf_op | source)
XLA Modules:
  0.0 60.4 jit_solution(2060128984523959074)
XLA Ops:
  0.0 58.8 %shard_map.64 = bf16[12,2,32,128]{3,2,1,0:T(8,128)(2,1)} custom-call(s32[8,6]{1,0:T(8,128)} %domain_ref.1, s32[2,12]{1,0:T(2,128)} %bitcast.2, s32[2,12]{1,0:T(2,128)} %bitcast.3, bf16[64,112,256]{2,1,0:T(8,128)(2,1)} %panels_ref.1, bf16[12,2,256,128]{3,2,1,0:T(8,128)(2,1)} %d_ref.1, bf16[12,2,128,128]{3,2,1,0:T(8,128)(2,1)} %c_ref.1), custom_call_target="tpu_custom_call" | custom-call | tf_op jit(solution)/shard_map/pallas_call | solution.py:183
  58.8 1.6 %copy.8 = bf16[12,2,32,128]{3,2,1,0:T(8,128)(2,1)} copy(bf16[12,2,32,128]{3,2,1,0:T(8,128)(2,1)} %shard_map.64) | data formatting | bytes 393216
